TPU v7x, 128 devices: a whole 4x4x4 slice. The times are simulated.
128 devices in a mesh: dp: 4 (over z), mp: 32 (over y, x, core).
Axes of the slice: x: 4, y: 4, z: 4, core: 2. Of those that a mesh axis runs over, the one named last changes fastest.
Arguments:
- tokens: bfloat16 [4096, 4096], P('dp', 'mp'), may hold values from -6 to 6
- decay: float32 [4096, 16], P('dp'), may hold values from 0.75 to 1, as said below
- state: float32 [128, 256, 8192], P('dp', None, 'mp'), may hold values from -24 to 24
- w_query: bfloat16 [4096, 4096], P(None, 'mp'), may hold values from -0.09375 to 0.09375
- w_key: bfloat16 [4096, 4096], P(None, 'mp'), may hold values from -0.09375 to 0.09375
- w_value: bfloat16 [4096, 8192], P(None, 'mp'), may hold values from -0.09375 to 0.09375
- w_gate: bfloat16 [4096, 8192], P(None, 'mp'), may hold values from -0.09375 to 0.09375
- w_out: bfloat16 [8192, 4096], P('mp'), may hold values from -0.125 to 0.125
- norm_gain: float32 [8192], P('mp'), may hold values from 0.25 to 1.75
Outputs:
- layer_out: bfloat16 [4096, 4096], P('dp', 'mp')
- new_state: float32 [128, 256, 8192], P('dp', None, 'mp')
Inputs may be any that keep to these rules, and one draw needn't show every extreme that they name: `decay`: each head has its own base rate over all tokens, varied somewhat from token to token.
All inputs are finite; a program needn't handle non-finite values.
Results may differ from a plain program's by a relative error of at most 0.0071.
Values may be sent and summed in bfloat16 or wider, within the bound.
No kernel may reach another device: no remote copies, remote signals or barrier semaphores. Data moves between devices by JAX's collectives and lax.ppermute only.
A program may use at most 128 MiB of HBM per device.

v0:
```python
import jax
import jax.numpy as jnp
from jax import lax
from jax.sharding import PartitionSpec as P

HEAD = 256
VHEAD = 512
NEW = 32
EPS = 0.1


def partner(shard, axis, bit):
    return lax.ppermute(shard, axis, [(i, i ^ 1 << bit) for i in range(lax.axis_size(axis))])


def per_device(tokens, decay, state, w_query, w_key, w_value, w_gate, w_out, norm_gain):
    tok_rows = tokens.shape[0]
    qk_columns = w_query.shape[1]
    v_columns = w_value.shape[1]
    groups = max(1, qk_columns // HEAD)
    qk_width = qk_columns // groups
    v_width = v_columns // groups
    sequences = tok_rows // NEW
    device_index = lax.axis_index("mp")
    first_head = device_index * qk_columns // HEAD
    qk_zeros = jnp.zeros((tok_rows, qk_columns), jnp.float32)
    v_zeros = jnp.zeros((tok_rows, v_columns), jnp.float32)
    carried = (qk_zeros, qk_zeros, v_zeros, v_zeros)
    segment = lax.all_gather(tokens, "mp", axis=1, tiled=True)
    updated = []
    for running, weight in zip(carried, (w_query, w_key, w_value, w_gate)):
        weight_rows = weight
        updated.append(jnp.dot(segment, weight_rows, preferred_element_type=jnp.float32))
    query, key_proj, value_proj, gate_proj = tuple(updated)
    query = (query * HEAD ** (-0.5)).astype(jnp.bfloat16).reshape(tok_rows, groups, qk_width)
    key_proj = key_proj.astype(jnp.bfloat16).reshape(tok_rows, groups, qk_width)
    value_proj = value_proj.astype(jnp.bfloat16)
    bit_number = 0
    other_query, other_key = partner((query, key_proj), "mp", bit_number)
    upper_half = device_index >> bit_number & 1 == 1
    query = jnp.where(
        upper_half,
        jnp.concatenate([other_query, query], 2),
        jnp.concatenate([query, other_query], 2),
    )
    key_proj = jnp.where(
        upper_half,
        jnp.concatenate([other_key, key_proj], 2),
        jnp.concatenate([key_proj, other_key], 2),
    )
    query_block = query.reshape(sequences, NEW, groups, HEAD)
    key_block = key_proj.reshape(sequences, NEW, groups, HEAD)
    value_block = value_proj.reshape(sequences, NEW, groups, v_width)
    decay_rates = lax.dynamic_slice_in_dim(decay, first_head, groups, 1).reshape(
        sequences, NEW, groups
    )
    log_cumul = jnp.cumsum(jnp.log(decay_rates), axis=1)
    old_state = state.reshape(sequences, HEAD, groups, v_width)
    from_state = jnp.einsum("bngk,bkgv->bngv", query_block.astype(jnp.float32), old_state)
    scores = jnp.einsum(
        "bngk,bmgk->bgnm", query_block, key_block, preferred_element_type=jnp.float32
    )
    along = jnp.transpose(log_cumul, (0, 2, 1))
    log_gap = along[:, :, :, None] - along[:, :, None, :]
    causal = jnp.arange(NEW)[:, None] >= jnp.arange(NEW)[None, :]
    factor = jnp.where(causal, jnp.exp(jnp.where(causal, log_gap, 0.0)), 0.0)
    weights = (scores * factor).astype(jnp.bfloat16)
    in_block = jnp.einsum(
        "bgnm,bmgv->bngv", weights, value_block, preferred_element_type=jnp.float32
    )
    retained = jnp.exp(log_cumul)[..., None] * from_state + in_block
    final_log = log_cumul[:, -1, :]
    carry_scale = jnp.exp(final_log[:, None, :] - log_cumul)
    decayed_keys = key_block.astype(jnp.float32) * carry_scale[..., None]
    fresh = jnp.einsum("bngk,bngv->bkgv", decayed_keys, value_block.astype(jnp.float32))
    new_state = jnp.exp(final_log)[:, None, :, None] * old_state + fresh
    new_state = new_state.reshape(sequences, HEAD, v_columns)
    retained = retained.reshape(tok_rows, groups, v_width)
    running = jnp.sum(retained, axis=-1)
    squares = jnp.sum(retained * retained, axis=-1)
    bit_number = 0
    other_sum, other_square = partner((running, squares), "mp", bit_number)
    running = running + other_sum
    squares = squares + other_square
    centre = running / VHEAD
    variance = squares / VHEAD - centre * centre
    deviation = retained - centre[..., None]
    normed = deviation * lax.rsqrt(variance + EPS)[..., None]
    gated_out = (normed.reshape(tok_rows, v_columns) * norm_gain * jax.nn.silu(gate_proj)).astype(
        jnp.bfloat16
    )
    out_cols = lax.all_to_all(w_out, "mp", split_axis=1, concat_axis=0, tiled=True)
    weight_rows = out_cols
    layer_out = jnp.dot(
        lax.all_gather(gated_out, "mp", axis=1, tiled=True),
        weight_rows,
        preferred_element_type=jnp.float32,
    ).astype(jnp.bfloat16)
    return (layer_out, new_state)


def solution(mesh):
    placed = (
        P("dp", "mp"),
        P("dp", None),
        P("dp", None, "mp"),
        P(None, "mp"),
        P(None, "mp"),
        P(None, "mp"),
        P(None, "mp"),
        P("mp", None),
        P("mp"),
    )
    return jax.shard_map(
        per_device,
        mesh=mesh,
        in_specs=placed,
        out_specs=(P("dp", "mp"), P("dp", None, "mp")),
        check_vma=False,
    )
```

profile of v0, /device:TPU:1, one launch (start us, length us, event | category | flops | bytes accessed | tf_op | source)
XLA Modules:
  0.0 216.4 jit_solution(17912909884485674575)
XLA Ops:
  7.2 0.7 all-gather.3.cloned.1.call-update
  8.0 0.8 log_reduce_fusion
  8.8 0.5 copy.22
  9.4 2.0 fusion.26
  11.4 0.4 copy.23
  11.7 0.1 slice_reduce_fusion
  11.9 0.1 subtract_exponential_fusion
  11.9 60.5 %all-gather.3.cloned.1.call-done = bf16[1024,4096]{1,0:T(8,128)(2,1)} async-done(((bf16[1024,128]{1,0:T(8,128)(2,1)}), bf16[1024,4096]{1,0:T(8,128)(2,1)}) %all-gather.3.cloned.1.call-update) | async-done | bytes 8388624 | tf_op jit(solution)/shard_map/all_gather | solution.py:29
  72.5 6.1 %fusion.4 = bf16[1024,128]{1,0:T(8,128)(2,1)S(1)} fusion(bf16[1024,4096]{1,0:T(8,128)(2,1)} %all-gather.3.cloned.1.call-done, bf16[4096,128]{1,0:T(8,128)(2,1)} %param.12), kind=kOutput, calls=%fused_computation.11 | convolution fusion | flops 1074003968 | bytes 9699328 | tf_op jit(solution)/shard_map/dot_general | solution.py:33
  78.5 0.3 collective-permute-start
  78.9 2.3 %convolution_convert_fusion.2 = bf16[1024,128]{1,0:T(8,128)(2,1)S(1)} fusion(bf16[1024,4096]{1,0:T(8,128)(2,1)S(1)} %copy-done.10, bf16[4096,128]{1,0:T(8,128)(2,1)S(1)} %copy-done.11), kind=kOutput, calls=%fused_computation.12 | convolution fusion | flops 1073872896 | bytes 9699328 | tf_op jit(solution)/shard_map/dot_general | solution.py:33
  81.2 0.3 collective-permute-start.1
  81.6 2.3 %convolution_convert_fusion = bf16[1024,256]{1,0:T(8,128)(2,1)S(1)} fusion(bf16[1024,4096]{1,0:T(8,128)(2,1)S(1)} %copy-done.10, bf16[4096,256]{1,0:T(8,128)(2,1)S(1)} %copy-done), kind=kOutput, calls=%fused_computation.6 | convolution fusion | flops 2147745792 | bytes 11010048 | tf_op jit(solution)/shard_map/dot_general | solution.py:33
  84.0 0.8 copy-done.8
  84.7 1.5 convolution_bitcast_fusion
  86.3 4.5 %fusion.9 = (f32[32,32]{1,0:T(8,128)S(1)}, f32[32,32]{1,0:T(8,128)S(1)}, f32[32,1,256,32]{2,3,0,1:T(8,128)S(1)}) fusion(f32[32,1,256,32]{2,3,0,1:T(8,128)S(1)} %convolution_bitcast_fusion, f32[32,256,256]{2,1,0:T(8,128)} %param.11, bf16[32,32,128]{2,1,0:T(8,128)(2,1)S(1)} %bitcast.72, bf16[32,32,128]{2,1,0:T(8,128)(2,1)} %bitcast.74, pred[]{:T(512)S(6)} %eq.3, ...), kind=kOutput, calls=%fused_computation.20 | convolution fusion | flops 137885696 | bytes 11022337 | tf_op jit(solution)/shard_map/bngk,bkgv->bngv/dot_general | solution.py:59
  90.8 0.1 reduce_sum.25
  90.9 0.1 reduce_sum.23
  91.0 0.3 collective-permute-start.2
  91.3 0.2 collective-permute-start.3
  91.5 0.7 collective-permute-done.2
  92.2 0.3 collective-permute-done.3
  92.5 7.4 %fusion.8 = bf16[1024,256]{1,0:T(8,128)(2,1)} fusion(f32[32,1,256,32]{2,3,0,1:T(8,128)S(1)} %get-tuple-element.14, f32[256]{0:T(256)S(1)} %copy-done.12, f32[1024]{0:T(1024)S(1)} %bitcast.81, f32[1024]{0:T(1024)S(1)} %bitcast.82, bf16[1024,4096]{1,0:T(8,128)(2,1)} %all-gather.3.cloned.1.call-done, bf16[4096,256]{1,0:T(8,128)(2,1)} %param.15), kind=kOutput, calls=%fused_computation.17 | convolution fusion | flops 2149842944 | bytes 12067840 | tf_op jit(solution)/shard_map/dot_general | solution.py:33
  99.9 2.5 %copy.24 = bf16[256,4096]{0,1:T(8,128)(2,1)} copy(bf16[256,4096]{1,0:T(8,128)(2,1)S(1)} %copy-done.2) | data formatting | bytes 4194304 | tf_op args[7]
  102.4 5.6 %all-to-all-start = ((bf16[256,32,128]{0,2,1:T(8,128)(2,1)}), bf16[256,32,128]{0,2,1:T(8,128)(2,1)S(1)}, u32[]{:S(2)}, u32[]{:S(2)}) async-start(bf16[256,32,128]{0,2,1:T(8,128)(2,1)} %bitcast.66), calls=%async_computation | async-start | bytes 4194304 | tf_op jit(solution)/shard_map/all_to_all | solution.py:92
  108.0 9.2 %copy.26 = f32[32,256,256]{1,2,0:T(8,128)} copy(f32[32,256,256]{2,1,0:T(8,128)} %param.11) | data formatting | bytes 16777216 | tf_op args[2]
  117.2 27.7 %all-to-all-done = bf16[256,32,128]{0,2,1:T(8,128)(2,1)S(1)} async-done(((bf16[256,32,128]{0,2,1:T(8,128)(2,1)}), bf16[256,32,128]{0,2,1:T(8,128)(2,1)S(1)}, u32[]{:S(2)}, u32[]{:S(2)}) %all-to-all-start) | async-done | bytes 2097184 | tf_op jit(solution)/shard_map/all_to_all | solution.py:92
  144.9 2.9 %copy.25 = bf16[32,256,128]{2,1,0:T(8,128)(2,1)} copy(bf16[32,256,128]{1,2,0:T(8,128)(2,1)S(1)} %bitcast.65) | data formatting | bytes 4194304 | tf_op jit(solution)/shard_map/all_to_all | solution.py:92
  147.8 8.5 %fusion = f32[32,256,256]{1,2,0:T(8,128)} fusion(f32[32,256,256]{1,2,0:T(8,128)} %copy.26, f32[32]{0:T(128)S(1)} %exp.38, bf16[32,32,256]{2,1,0:T(8,128)(2,1)S(1)} %bitcast.69, f32[32,32]{1,0:T(8,128)S(1)} %get-tuple-element.12, bf16[32,32,128]{2,1,0:T(8,128)(2,1)S(1)} %bitcast.77, bf16[32,32,128]{2,1,0:T(8,128)(2,1)S(1)} %bitcast.79, pred[]{:T(512)S(6)} %eq.3), kind=kOutput, calls=%fused_computation.1 | convolution fusion | flops 141295616 | bytes 17830016 | tf_op jit(solution)/shard_map/bngk,bngv->bkgv/dot_general | solution.py:75
  156.3 9.0 %copy.27 = f32[32,256,256]{2,1,0:T(8,128)} copy(f32[32,256,256]{1,2,0:T(8,128)} %fusion) | data formatting | bytes 16777216
  165.3 32.6 %all-gather.5.cloned.1.call-done = bf16[1024,8192]{1,0:T(8,128)(2,1)} async-done(((bf16[1024,256]{1,0:T(8,128)(2,1)}), bf16[1024,8192]{1,0:T(8,128)(2,1)}) %all-gather.5.cloned.1.call-update) | async-done | bytes 16777232 | tf_op jit(solution)/shard_map/all_gather | solution.py:95
  197.9 11.7 %convolution_convert_fusion.1 = bf16[1024,128]{1,0:T(8,128)(2,1)} fusion(bf16[1024,8192]{1,0:T(8,128)(2,1)} %all-gather.5.cloned.1.call-done, bf16[8192,128]{1,0:T(8,128)(2,1)} %bitcast.67), kind=kOutput, calls=%fused_computation.9 | convolution fusion | flops 2147614720 | bytes 19136512 | tf_op jit(solution)/shard_map/dot_general | solution.py:94
  (34 shorter events, 0.3 us)
Async XLA Ops:
  7.2 74.4 %copy-start = (bf16[4096,256]{1,0:T(8,128)(2,1)S(1)}, bf16[4096,256]{1,0:T(8,128)(2,1)}, u32[]{:S(2)}) copy-start(bf16[4096,256]{1,0:T(8,128)(2,1)} %param.14) | copy-start | bytes 6291460
  7.2 65.3 %all-gather.3.cloned.1.call-start = ((), (), s32[]{:S(2)}) async-start(), calls=%async_computation.1 | async-start | bytes 8650752 | tf_op jit(solution)/shard_map/all_gather | solution.py:29
  7.9 190.0 %all-gather.5.cloned.1.call-start = ((), (), s32[]{:S(2)}) async-start(), calls=%async_computation.2 | async-start | bytes 17301504 | tf_op jit(solution)/shard_map/all_gather | solution.py:95
  72.5 6.4 %copy-start.10 = (bf16[1024,4096]{1,0:T(8,128)(2,1)S(1)}, bf16[1024,4096]{1,0:T(8,128)(2,1)}, u32[]{:S(2)}) copy-start(bf16[1024,4096]{1,0:T(8,128)(2,1)} %all-gather.3.cloned.1.call-done) | copy-start | bytes 25165828
  72.5 6.4 %copy-start.11 = (bf16[4096,128]{1,0:T(8,128)(2,1)S(1)}, bf16[4096,128]{1,0:T(8,128)(2,1)}, u32[]{:S(2)}) copy-start(bf16[4096,128]{1,0:T(8,128)(2,1)} %param.13) | copy-start | bytes 3145732
  78.5 5.4 %collective-permute-start = (bf16[1024,1,128]{2,0,1:T(8,128)(2,1)S(1)}, bf16[1024,1,128]{2,0,1:T(8,128)(2,1)S(1)}, u32[]{:S(2)}, u32[]{:S(2)}) collective-permute-start(bf16[1024,1,128]{2,0,1:T(8,128)(2,1)S(1)} %bitcast.70), channel_id=1, source_target_pairs={{0,1},{1,0},{2,3},{3,2},{4,5},{5,4},{6,7},{7,6},{8,9},{9,8},{10,11... | collective-permute-start | bytes 786440 | tf_op jit(solution)/shard_map/ppermute | solution.py:13
  81.2 5.0 %copy-start.6 = (bf16[1024,128]{1,0:T(8,128)(2,1)}, bf16[1024,128]{1,0:T(8,128)(2,1)S(1)}, u32[]{:S(2)}) copy-start(bf16[1024,128]{1,0:T(8,128)(2,1)S(1)} %convolution_convert_fusion.2) | copy-start | bytes 786436
  81.2 2.7 %collective-permute-start.1 = (bf16[1024,1,128]{2,0,1:T(8,128)(2,1)S(1)}, bf16[1024,1,128]{2,0,1:T(8,128)(2,1)S(1)}, u32[]{:S(2)}, u32[]{:S(2)}) collective-permute-start(bf16[1024,1,128]{2,0,1:T(8,128)(2,1)S(1)} %bitcast.75), channel_id=1, source_target_pairs={{0,1},{1,0},{2,3},{3,2},{4,5},{5,4},{6,7},{7,6},{8,9},{9,8},{10,11... | collective-permute-start | bytes 786440 | tf_op jit(solution)/shard_map/ppermute | solution.py:13
  83.9 2.4 %copy-start.3 = (bf16[1024,256]{1,0:T(8,128)(2,1)}, bf16[1024,256]{1,0:T(8,128)(2,1)S(1)}, u32[]{:S(2)}) copy-start(bf16[1024,256]{1,0:T(8,128)(2,1)S(1)} %convolution_convert_fusion) | copy-start | bytes 1572868
  83.9 2.4 %copy-start.5 = (bf16[1024,1,128]{2,0,1:T(8,128)(2,1)}, bf16[1024,1,128]{2,0,1:T(8,128)(2,1)S(1)}, u32[]{:S(2)}) copy-start(bf16[1024,1,128]{2,0,1:T(8,128)(2,1)S(1)} %collective-permute-done) | copy-start | bytes 786436
  84.0 0.8 copy-start.8
  84.7 7.8 %copy-start.12 = (f32[256]{0:T(256)S(1)}, f32[256]{0:T(256)}, u32[]{:S(2)}) copy-start(f32[256]{0:T(256)} %param.17) | copy-start | bytes 3076
  91.0 1.2 collective-permute-start.2
  91.3 1.2 collective-permute-start.3
  92.5 7.4 %copy-start.2 = (bf16[256,4096]{1,0:T(8,128)(2,1)S(1)}, bf16[256,4096]{1,0:T(8,128)(2,1)}, u32[]{:S(2)}) copy-start(bf16[256,4096]{1,0:T(8,128)(2,1)} %param.16) | copy-start | bytes 6291460
  102.4 42.5 %all-to-all-start = ((bf16[256,32,128]{0,2,1:T(8,128)(2,1)}), bf16[256,32,128]{0,2,1:T(8,128)(2,1)S(1)}, u32[]{:S(2)}, u32[]{:S(2)}) async-start(bf16[256,32,128]{0,2,1:T(8,128)(2,1)} %bitcast.66), calls=%async_computation | async-start | bytes 4194304 | tf_op jit(solution)/shard_map/all_to_all | solution.py:92
  108.0 39.8 %copy-start.4 = (bf16[1024,256]{1,0:T(8,128)(2,1)S(1)}, bf16[1024,256]{1,0:T(8,128)(2,1)}, u32[]{:S(2)}) copy-start(bf16[1024,256]{1,0:T(8,128)(2,1)} %copy-done.3) | copy-start | bytes 1572868
  108.0 39.8 %copy-start.7 = (bf16[1024,128]{1,0:T(8,128)(2,1)S(1)}, bf16[1024,128]{1,0:T(8,128)(2,1)}, u32[]{:S(2)}) copy-start(bf16[1024,128]{1,0:T(8,128)(2,1)} %copy-done.6) | copy-start | bytes 786436
  108.0 39.8 %copy-start.9 = (bf16[1024,1,128]{2,0,1:T(8,128)(2,1)S(1)}, bf16[1024,1,128]{2,0,1:T(8,128)(2,1)}, u32[]{:S(2)}) copy-start(bf16[1024,1,128]{2,0,1:T(8,128)(2,1)} %copy-done.8) | copy-start | bytes 786436
  197.9 11.7 %copy-start.1 = (bf16[4096,256]{1,0:T(8,128)(2,1)S(1)}, bf16[4096,256]{1,0:T(8,128)(2,1)}, u32[]{:S(2)}) copy-start(bf16[4096,256]{1,0:T(8,128)(2,1)} %param.14) | copy-start | bytes 6291460
Sparse Core Ops, SparseCore 0:
  10.2 62.2 all-gather.2
  100.0 97.8 all-gather.4
where the time goes:
time: 217 us; the launch traced here: 216 us
  waiting for transfers between devices  122 us (56%)
  matrix products  44.4 us (20%)
  local copies, waits for them, and re-layouts  26.4 us (12%)
  between operations  14.3 us (7%)
  starting transfers between devices  6.87 us (3%)
    all_gather x1, waiting for transfers between devices, per_device(): segment = lax.all_gather(tokens, 'mp', axis=1, tiled=True)  60.5 us
    all_gather x1, waiting for transfers between devices, per_device(): lax.all_gather(gated_out, 'mp', axis=1, tiled=True)  32.6 us
    all_to_all x1, waiting for transfers between devices, per_device(): lax.all_to_all(w_out, 'mp', split_axis=1, concat_axis=0, tiled=True)  27.7 us
    unnamed x29, local copies, waits for them, and re-layouts  21.5 us
    dot_general x4, matrix products, per_device(): jnp.dot(segment, weight_rows, preferred_element_type=jnp.float32)  18.1 us
    dot_general x1, matrix products, per_device(): jnp.dot(lax.all_gather(gated_out, 'mp', axis=1, tiled=True), weight_rows,...  11.7 us
    dot_general x1, matrix products, per_device(): jnp.einsum('bngk,bngv->bkgv', decayed_keys, value_block.astype(jnp.float32))  8.48 us
    all_to_all x1, starting transfers between devices, per_device(): lax.all_to_all(w_out, 'mp', split_axis=1, concat_axis=0, tiled=True)  5.6 us
  transfers between devices with their start and end apart: 7, of which 5 were waited for; matrix products, arithmetic and copies ran while one was open for 19% of the time, Pallas kernels for 0%

commit v1 on v0

--- a/solution.py
+++ b/solution.py
@@ -7,6 +7,12 @@
 VHEAD = 512
 NEW = 32
 EPS = 0.1
+
+
+def halves_draw(original):
+    met_up = jnp.stack([original for _ in range(lax.axis_size("mp"))], axis=0)
+    local_out = lax.all_to_all(met_up, "mp", 0, 0)
+    return jnp.concatenate(local_out, axis=1)
 
 
 def partner(shard, axis, bit):
@@ -92,9 +98,7 @@
     out_cols = lax.all_to_all(w_out, "mp", split_axis=1, concat_axis=0, tiled=True)
     weight_rows = out_cols
     layer_out = jnp.dot(
-        lax.all_gather(gated_out, "mp", axis=1, tiled=True),
-        weight_rows,
-        preferred_element_type=jnp.float32,
+        halves_draw(gated_out), weight_rows, preferred_element_type=jnp.float32
     ).astype(jnp.bfloat16)
     return (layer_out, new_state)
 

time: 217 us -> 360 us (1.66)
  the two profiles are of different devices: /device:TPU:1 before, /device:TPU:0 now
where the time goes in v1:
time: 360 us; the launch traced here: 359 us
  waiting for transfers between devices  250 us (69%)
  matrix products  42.6 us (12%)
  local copies, waits for them, and re-layouts  34.9 us (10%)
  starting transfers between devices  14.7 us (4%)
  between operations  14.2 us (4%)
    all_to_all x1, waiting for transfers between devices, halves_draw(): local_out = lax.all_to_all(met_up, 'mp', 0, 0)  187 us
    all_gather x1, waiting for transfers between devices, per_device(): segment = lax.all_gather(tokens, 'mp', axis=1, tiled=True)  61.6 us
    unnamed x17, local copies, waits for them, and re-layouts  22.9 us
    dot_general x4, matrix products, per_device(): jnp.dot(segment, weight_rows, preferred_element_type=jnp.float32)  17.2 us
    dot_general x1, matrix products, per_device(): jnp.dot(halves_draw(gated_out), weight_rows, preferred_element_type=jnp.f...  11.6 us
    dot_general x1, matrix products, per_device(): jnp.einsum('bngk,bngv->bkgv', decayed_keys, value_block.astype(jnp.float32))  7.98 us
    all_to_all x1, starting transfers between devices, per_device(): lax.all_to_all(w_out, 'mp', split_axis=1, concat_axis=0, tiled=True)  7.56 us
  transfers between devices with their start and end apart: 7, of which 4 were waited for; matrix products, arithmetic and copies ran while one was open for 17% of the time, Pallas kernels for 0%

profile of v1, /device:TPU:0, one launch (start us, length us, event | category | flops | bytes accessed | tf_op | source)
XLA Modules:
  0.0 358.9 jit_solution(11488868237713420716)
XLA Ops:
  7.2 0.7 all-gather.2.cloned.1.call-update
  7.9 4.1 %copy.20 = bf16[256,4096]{0,1:T(8,128)(2,1)} copy(bf16[256,4096]{1,0:T(8,128)(2,1)} %param.16) | data formatting | bytes 4194304 | tf_op args[7]
  12.0 4.1 %copy.21 = bf16[256,32,128]{2,0,1:T(8,128)(2,1)} copy(bf16[256,32,128]{0,2,1:T(8,128)(2,1)} %bitcast.79) | data formatting | bytes 4194304 | tf_op jit(solution)/shard_map/all_to_all | solution.py:98
  16.0 7.6 %all-to-all-start.1 = ((bf16[256,32,128]{2,0,1:T(8,128)(2,1)}), bf16[256,32,128]{2,0,1:T(8,128)(2,1)}, u32[]{:S(2)}, u32[]{:S(2)}) async-start(bf16[256,32,128]{2,0,1:T(8,128)(2,1)} %copy.21), calls=%async_computation.1 | async-start | bytes 4194304 | tf_op jit(solution)/shard_map/all_to_all | solution.py:98
  23.6 0.8 log_reduce_fusion
  24.5 0.5 copy.18
  25.0 2.0 fusion.39
  27.0 0.4 copy.19
  27.4 0.1 slice_reduce_fusion
  27.6 61.6 %all-gather.2.cloned.1.call-done = bf16[1024,4096]{1,0:T(8,128)(2,1)} async-done(((bf16[1024,128]{1,0:T(8,128)(2,1)}), bf16[1024,4096]{1,0:T(8,128)(2,1)}) %all-gather.2.cloned.1.call-update) | async-done | bytes 8388624 | tf_op jit(solution)/shard_map/all_gather | solution.py:35
  89.2 6.1 %convolution_convert_fusion.1 = bf16[1024,128]{1,0:T(8,128)(2,1)S(1)} fusion(bf16[1024,4096]{1,0:T(8,128)(2,1)} %all-gather.2.cloned.1.call-done, bf16[4096,128]{1,0:T(8,128)(2,1)} %param.13), kind=kOutput, calls=%fused_computation.15 | convolution fusion | flops 1073872896 | bytes 9699328 | tf_op jit(solution)/shard_map/dot_general | solution.py:39
  95.3 0.3 collective-permute-start.1
  95.6 2.3 fusion.12
  97.9 0.3 collective-permute-start
  98.3 2.3 convolution_convert_fusion
  100.6 0.7 copy-done.2
  101.3 1.6 convolution_bitcast_fusion
  102.9 4.4 %fusion.22 = (f32[32,32]{1,0:T(8,128)S(1)}, f32[32,32]{1,0:T(8,128)S(1)}, f32[32,1,256,32]{2,3,0,1:T(8,128)S(1)}) fusion(f32[32,1,256,32]{2,3,0,1:T(8,128)S(1)} %convolution_bitcast_fusion, f32[32,256,256]{2,1,0:T(8,128)} %param.11, bf16[32,32,128]{2,1,0:T(8,128)(2,1)S(1)} %bitcast.84, bf16[32,32,128]{2,1,0:T(8,128)(2,1)S(1)} %bitcast.86, pred[]{:T(512)S(6)} %eq.3, ...), kind=kOutput, calls=%fused_computation.24 | convolution fusion | flops 137885696 | bytes 11022337 | tf_op jit(solution)/shard_map/bngk,bkgv->bngv/dot_general | solution.py:65
  107.3 0.1 reduce_sum.25
  107.3 0.3 collective-permute-start.3
  107.6 0.1 reduce_sum.23
  107.7 0.5 collective-permute-start.2
  108.1 0.4 collective-permute-done.3
  108.5 0.5 collective-permute-done.2
  109.1 6.4 %fusion.21 = bf16[1024,256]{1,0:T(8,128)(2,1)S(1)} fusion(f32[32,1,256,32]{2,3,0,1:T(8,128)S(1)} %get-tuple-element.12, f32[256]{0:T(256)S(1)} %copy-done.6, f32[1024]{0:T(1024)S(1)} %bitcast.93, f32[1024]{0:T(1024)S(1)} %bitcast.94, bf16[1024,4096]{1,0:T(8,128)(2,1)} %all-gather.2.cloned.1.call-done, bf16[4096,256]{1,0:T(8,128)(2,1)} %param.15), kind=kOutput, calls=%fused_computation.21 | convolution fusion | flops 2149842944 | bytes 12067840 | tf_op jit(solution)/shard_map/dot_general | solution.py:39
  115.5 6.0 %stack.2 = bf16[32,1024,256]{2,1,0:T(8,128)(2,1)} broadcast(bf16[1024,256]{1,0:T(8,128)(2,1)S(1)} %fusion.21), dimensions={1,2} | broadcast | bytes 17301504 | tf_op jit(solution)/shard_map/stack | solution.py:13
  121.5 5.7 %all-to-all-start = ((bf16[32,1024,256]{2,1,0:T(8,128)(2,1)}), bf16[32,1024,256]{2,1,0:T(8,128)(2,1)}, u32[]{:S(2)}, u32[]{:S(2)}) async-start(bf16[32,1024,256]{2,1,0:T(8,128)(2,1)} %stack.2), calls=%async_computation | async-start | bytes 33554432 | tf_op jit(solution)/shard_map/all_to_all | solution.py:14
  127.2 9.0 %copy.22 = f32[32,256,256]{1,2,0:T(8,128)} copy(f32[32,256,256]{2,1,0:T(8,128)} %param.11) | data formatting | bytes 16777216 | tf_op args[2]
  136.2 8.0 %fusion.2 = f32[32,256,256]{1,2,0:T(8,128)} fusion(f32[32,256,256]{1,2,0:T(8,128)} %copy.22, f32[32]{0:T(128)S(1)} %exp.38, bf16[32,32,256]{2,1,0:T(8,128)(2,1)S(1)} %bitcast.81, f32[32,32]{1,0:T(8,128)S(1)} %get-tuple-element.10, bf16[32,32,128]{2,1,0:T(8,128)(2,1)S(1)} %bitcast.89, bf16[32,32,128]{2,1,0:T(8,128)(2,1)S(1)} %bitcast.91, pred[]{:T(512)S(6)} %eq.3), kind=kOutput, calls=%fused_computation.3 | convolution fusion | flops 141295616 | bytes 17830016 | tf_op jit(solution)/shard_map/bngk,bngv->bkgv/dot_general | solution.py:81
  144.2 9.1 %copy.23 = f32[32,256,256]{2,1,0:T(8,128)} copy(f32[32,256,256]{1,2,0:T(8,128)} %fusion.2) | data formatting | bytes 16777216
  153.3 187.2 %all-to-all-done = bf16[32,1024,256]{2,1,0:T(8,128)(2,1)} async-done(((bf16[32,1024,256]{2,1,0:T(8,128)(2,1)}), bf16[32,1024,256]{2,1,0:T(8,128)(2,1)}, u32[]{:S(2)}, u32[]{:S(2)}) %all-to-all-start) | async-done | bytes 16777248 | tf_op jit(solution)/shard_map/all_to_all | solution.py:14
  340.5 11.6 %fusion.13 = bf16[1024,128]{1,0:T(8,128)(2,1)} fusion(bf16[256,32,128]{2,0,1:T(8,128)(2,1)} %all-to-all-done.1, bf16[32,1024,256]{2,1,0:T(8,128)(2,1)} %all-to-all-done), kind=kOutput, calls=%fused_computation.16 | convolution fusion | flops 2147614720 | bytes 19136512 | tf_op jit(solution)/shard_map/dot_general | solution.py:100
  (22 shorter events, 0.3 us)
Async XLA Ops:
  7.2 91.1 %copy-start = (bf16[4096,256]{1,0:T(8,128)(2,1)S(1)}, bf16[4096,256]{1,0:T(8,128)(2,1)}, u32[]{:S(2)}) copy-start(bf16[4096,256]{1,0:T(8,128)(2,1)} %param.14) | copy-start | bytes 6291460
  7.2 82.0 %all-gather.2.cloned.1.call-start = ((), (), s32[]{:S(2)}) async-start(), calls=%async_computation.2 | async-start | bytes 8650752 | tf_op jit(solution)/shard_map/all_gather | solution.py:35
  16.0 99.5 %all-to-all-start.1 = ((bf16[256,32,128]{2,0,1:T(8,128)(2,1)}), bf16[256,32,128]{2,0,1:T(8,128)(2,1)}, u32[]{:S(2)}, u32[]{:S(2)}) async-start(bf16[256,32,128]{2,0,1:T(8,128)(2,1)} %copy.21), calls=%async_computation.1 | async-start | bytes 4194304 | tf_op jit(solution)/shard_map/all_to_all | solution.py:98
  89.2 6.4 %copy-start.4 = (bf16[1024,4096]{1,0:T(8,128)(2,1)S(1)}, bf16[1024,4096]{1,0:T(8,128)(2,1)}, u32[]{:S(2)}) copy-start(bf16[1024,4096]{1,0:T(8,128)(2,1)} %all-gather.2.cloned.1.call-done) | copy-start | bytes 25165828
  89.2 6.4 %copy-start.5 = (bf16[4096,128]{1,0:T(8,128)(2,1)S(1)}, bf16[4096,128]{1,0:T(8,128)(2,1)}, u32[]{:S(2)}) copy-start(bf16[4096,128]{1,0:T(8,128)(2,1)} %param.12) | copy-start | bytes 3145732
  95.3 5.4 %collective-permute-start.1 = (bf16[1024,1,128]{2,0,1:T(8,128)(2,1)S(1)}, bf16[1024,1,128]{2,0,1:T(8,128)(2,1)S(1)}, u32[]{:S(2)}, u32[]{:S(2)}) collective-permute-start(bf16[1024,1,128]{2,0,1:T(8,128)(2,1)S(1)} %bitcast.87), channel_id=1, source_target_pairs={{0,1},{1,0},{2,3},{3,2},{4,5},{5,4},{6,7},{7,6},{8,9},{9,8},{10,11... | collective-permute-start | bytes 786440 | tf_op jit(solution)/shard_map/ppermute | solution.py:19
  97.9 2.7 collective-permute-start
  100.6 0.7 copy-start.2
  101.3 7.7 %copy-start.6 = (f32[256]{0:T(256)S(1)}, f32[256]{0:T(256)}, u32[]{:S(2)}) copy-start(f32[256]{0:T(256)} %param.17) | copy-start | bytes 3076
  107.3 1.2 collective-permute-start.3
  107.7 1.4 collective-permute-start.2
  121.5 219.0 %all-to-all-start = ((bf16[32,1024,256]{2,1,0:T(8,128)(2,1)}), bf16[32,1024,256]{2,1,0:T(8,128)(2,1)}, u32[]{:S(2)}, u32[]{:S(2)}) async-start(bf16[32,1024,256]{2,1,0:T(8,128)(2,1)} %stack.2), calls=%async_computation | async-start | bytes 33554432 | tf_op jit(solution)/shard_map/all_to_all | solution.py:14
  127.2 9.0 %copy-start.3 = (bf16[1024,1,128]{2,0,1:T(8,128)(2,1)S(1)}, bf16[1024,1,128]{2,0,1:T(8,128)(2,1)}, u32[]{:S(2)}) copy-start(bf16[1024,1,128]{2,0,1:T(8,128)(2,1)} %copy-done.2) | copy-start | bytes 786436
  144.2 207.8 %copy-start.1 = (bf16[4096,256]{1,0:T(8,128)(2,1)S(1)}, bf16[4096,256]{1,0:T(8,128)(2,1)}, u32[]{:S(2)}) copy-start(bf16[4096,256]{1,0:T(8,128)(2,1)} %param.14) | copy-start | bytes 6291460
Sparse Core Ops, SparseCore 0:
  10.2 78.9 all-gather.1
